TPU v7x, 32 devices: a whole 2x2x4 slice. The times are simulated.
32 devices in a mesh: ctx: 16 (over z, x, core), tp: 2 (over y).
Axes of the slice: x: 2, y: 2, z: 4, core: 2. Of those that a mesh axis runs over, the one named last changes fastest.
Arguments:
- token_ids: int32 [12288], P('ctx'), may hold values from 0 to 511
- embed_table: bfloat16 [512, 4096], replicated, may hold values from -6 to 6
- norm_gain: float32 [4096], replicated, may hold values from 0.25 to 1.75
- w_in: bfloat16 [4096, 3, 2048], P(None, None, 'tp'), may hold values from -0.09375 to 0.09375
- short_taps: float32 [3, 3, 2048], P(None, None, 'tp'), may hold values from -3 to 3
- long_filter: bfloat16 [2048, 12288], P('tp', 'ctx'), may hold values from -0.0546875 to 0.0546875
- skip_gain: float32 [2048], P('tp'), may hold values from 0.5 to 2
- w_out: bfloat16 [2048, 4096], P(None, 'tp'), may hold values from -0.125 to 0.125
Outputs:
- mixed: bfloat16 [12288, 4096], P('ctx', 'tp')
All inputs are finite; a program needn't handle non-finite values.
Results may differ from a plain program's by a relative error of at most 0.0095.
Values may be sent and summed in bfloat16 or wider, within the bound.
A program may use at most 192 MiB of HBM per device.

v0:
```python
import math
import jax
import jax.numpy as jnp
from jax import lax
from jax.sharding import PartitionSpec as P

norm_eps = 1e-06


def shifted(block, axis, distance):
    devices = range(lax.axis_size(axis))
    route = [(i - distance, i) for i in devices if i - distance in devices]
    return lax.ppermute(block, axis, route)


def angle_table(outer, inner, period):
    product = (
        jnp.arange(outer, dtype=jnp.int32)[:, None]
        * jnp.arange(inner, dtype=jnp.int32)[None, :]
        % period
    )
    phase = product.astype(jnp.float32) * (2.0 * math.pi / period)
    return (jnp.cos(phase), jnp.sin(phase))


def contract(form, left, right):
    return jnp.einsum(
        form, left, right, precision=lax.Precision.HIGHEST, preferred_element_type=jnp.float32
    )


def forward_transform(signal, tables):
    cos_rows, sin_rows, cos_twist, sin_twist, cos_cols, sin_cols = tables
    first_real = contract("kn,cnm->ckm", cos_rows, signal)
    first_imag = -contract("kn,cnm->ckm", sin_rows, signal)
    turned_real = first_real * cos_twist + first_imag * sin_twist
    turned_imag = first_imag * cos_twist - first_real * sin_twist
    spec_real = contract("ckm,mj->ckj", turned_real, cos_cols) + contract(
        "ckm,mj->ckj", turned_imag, sin_cols
    )
    spec_imag = contract("ckm,mj->ckj", turned_imag, cos_cols) - contract(
        "ckm,mj->ckj", turned_real, sin_cols
    )
    return (spec_real, spec_imag)


def inverse_transform(spec_real, spec_imag, tables, period):
    cos_rows, sin_rows, cos_twist, sin_twist, cos_cols, sin_cols = tables
    back_real = contract("ckj,mj->ckm", spec_real, cos_cols) - contract(
        "ckj,mj->ckm", spec_imag, sin_cols
    )
    back_imag = contract("ckj,mj->ckm", spec_imag, cos_cols) + contract(
        "ckj,mj->ckm", spec_real, sin_cols
    )
    untwist_real = back_real * cos_twist - back_imag * sin_twist
    untwist_imag = back_imag * cos_twist + back_real * sin_twist
    signal = contract("kn,ckm->cnm", cos_rows, untwist_real) - contract(
        "kn,ckm->cnm", sin_rows, untwist_imag
    )
    return signal / period


def causal_conv(signal, kernel):
    channels = signal.shape[0]
    length = signal.shape[1]
    col_count = min(256, length)
    row_count = 2 * length // col_count
    half_rows = length // col_count
    cos_rows, sin_rows = angle_table(row_count, half_rows, row_count)
    cos_twist, sin_twist = angle_table(row_count, col_count, row_count * col_count)
    cos_cols, sin_cols = angle_table(col_count, col_count, col_count)
    tables = (cos_rows, sin_rows, cos_twist, sin_twist, cos_cols, sin_cols)
    signal_real, signal_imag = forward_transform(
        signal.astype(jnp.float32).reshape(channels, half_rows, col_count), tables
    )
    kernel_real, kernel_imag = forward_transform(
        kernel.astype(jnp.float32).reshape(channels, half_rows, col_count), tables
    )
    joint_real = signal_real * kernel_real - signal_imag * kernel_imag
    joint_imag = signal_real * kernel_imag + signal_imag * kernel_real
    result = inverse_transform(joint_real, joint_imag, tables, row_count * col_count)
    return result.reshape(channels, length)


def local(token_ids, embed_table, norm_gain, w_in, short_taps, long_filter, skip_gain, w_out):
    vocab = embed_table.shape[0]
    one_hot = (token_ids[:, None] == jnp.arange(vocab, dtype=jnp.int32)[None, :]).astype(
        jnp.bfloat16
    )
    embedded = jnp.dot(one_hot, embed_table, preferred_element_type=jnp.float32)
    scale = lax.rsqrt(jnp.mean(embedded * embedded, axis=1, keepdims=True) + norm_eps)
    normed = (embedded * scale * norm_gain).astype(jnp.bfloat16)
    width = w_in.shape[0]
    chan_part = w_in.shape[2]
    flat_proj = jnp.dot(
        normed, w_in.reshape(width, 3 * chan_part), preferred_element_type=jnp.float32
    ).astype(jnp.bfloat16)
    projected = jnp.transpose(flat_proj.reshape(-1, 3, chan_part), (1, 2, 0))
    positions = projected.shape[2]
    edge = projected[:, :, positions - 2 :]
    prior = shifted(edge, "ctx", 1)
    extended = jnp.concatenate([prior, projected], axis=2).astype(jnp.float32)
    shortened = (
        short_taps[0][:, :, None] * extended[:, :, 2:]
        + short_taps[1][:, :, None] * extended[:, :, 1 : positions + 1]
        + short_taps[2][:, :, None] * extended[:, :, 0:positions]
    ).astype(jnp.bfloat16)
    query_side = shortened[0]
    key_side = shortened[1]
    value_side = shortened[2]
    local_channels = shortened.shape[1]
    groups = lax.axis_size("ctx")
    owned = local_channels // groups

    def spread(array):
        return array.reshape(groups, owned, array.shape[-1])

    first_channel = lax.axis_index("ctx") * owned
    own_skip = lax.dynamic_slice_in_dim(skip_gain, first_channel, owned)[:, None]
    product_local = (key_side.astype(jnp.float32) * value_side.astype(jnp.float32)).astype(
        jnp.bfloat16
    )
    arrived = (
        lax.all_to_all(spread(product_local), "ctx", split_axis=0, concat_axis=2, tiled=True),
        lax.all_to_all(spread(long_filter), "ctx", split_axis=0, concat_axis=2, tiled=True),
    )
    product = arrived[0].reshape(owned, -1)
    filter_full = arrived[1].reshape(owned, -1)
    convolved = causal_conv(product, filter_full)
    outgoing = (convolved + own_skip * product.astype(jnp.float32)).astype(jnp.bfloat16)
    returned = lax.all_to_all(
        outgoing.reshape(1, owned, -1), "ctx", split_axis=2, concat_axis=0, tiled=True
    )
    returned = returned.reshape(local_channels, positions)
    gated = (query_side.astype(jnp.float32) * returned.astype(jnp.float32)).astype(jnp.bfloat16)
    width_part = w_out.shape[1]
    projected_out = jnp.dot(
        lax.all_gather(gated, "tp", axis=0, tiled=True).T, w_out, preferred_element_type=jnp.float32
    )
    residual = lax.dynamic_slice_in_dim(embedded, lax.axis_index("tp") * width_part, width_part, 1)
    return (residual + projected_out).astype(jnp.bfloat16)


def solution(mesh):
    return jax.shard_map(
        local,
        mesh=mesh,
        in_specs=(
            P("ctx"),
            P(),
            P(),
            P(None, None, "tp"),
            P(None, None, "tp"),
            P("tp", "ctx"),
            P("tp"),
            P(None, "tp"),
        ),
        out_specs=P("ctx", "tp"),
        check_vma=False,
    )
```

profile of v0, /device:TPU:0, one launch (start us, length us, event | category | flops | bytes accessed | tf_op | source)
XLA Modules:
  0.0 508.5 jit_solution(8029366977371177981)
XLA Ops:
  6.5 7.4 %all-to-all-start.1 = ((bf16[16,64,768]{2,1,0:T(8,128)(2,1)}), bf16[16,64,768]{2,1,0:T(8,128)(2,1)S(1)}, u32[]{:S(2)}, u32[]{:S(2)}) async-start(bf16[16,64,768]{2,1,0:T(8,128)(2,1)} %bitcast.149), calls=%async_computation.1 | async-start | bytes 3145728 | tf_op jit(solution)/shard_map/all_to_all | solution.py:125
  13.9 8.8 %multiply_reduce_fusion = (f32[768]{0:T(1024)S(1)}, f32[768,4096]{1,0:T(8,128)}) fusion(bf16[512,4096]{1,0:T(8,128)(2,1)} %param.9, s32[768]{0:T(1024)} %param.8), kind=kOutput, calls=%fused_computation.1 | convolution fusion | flops 3227909376 | bytes 16783360 | tf_op jit(solution)/shard_map/dot_general | solution.py:90
  22.7 33.5 %copy.32 = bf16[4096,3,1024]{0,2,1:T(8,128)(2,1)} copy(bf16[4096,3,1024]{2,0,1:T(8,128)(2,1)} %param.11) | data formatting | bytes 50331648 | tf_op args[3]
  56.2 27.9 %fusion.24 = bf16[768,3072]{1,0:T(8,128)(2,1)} fusion(bf16[4096,3072]{0,1:T(8,128)(2,1)} %bitcast.138, f32[768,4096]{1,0:T(8,128)} %get-tuple-element.11, f32[4096]{0:T(1024)S(1)} %copy-done.9, f32[768]{0:T(1024)S(1)} %add_rsqrt_fusion), kind=kOutput, calls=%fused_computation.39 | convolution fusion | flops 19339149312 | bytes 42486784 | tf_op jit(solution)/shard_map/dot_general | solution.py:95
  84.1 6.6 %copy.33 = bf16[768,3072]{0,1:T(8,128)(2,1)} copy(bf16[768,3072]{1,0:T(8,128)(2,1)} %fusion.24) | data formatting | bytes 9437184 | tf_op jit(solution)/shard_map/convert_element_type | solution.py:97
  90.7 1.4 slice.40
  92.2 0.3 copy.34
  92.5 2.6 collective-permute-start
  95.1 0.4 fusion.86
  95.5 0.8 dynamic_slice.7
  96.3 0.0 collective-permute-done
  96.3 0.4 copy.35
  96.7 4.8 maximum_convert_fusion
  101.5 8.1 %fusion.1 = bf16[3,1024,768]{2,1,0:T(8,128)(2,1)S(1)} fusion(f32[3,1024,770]{2,1,0:T(8,128)S(1)} %maximum_convert_fusion, f32[3,1024]{1,0:T(4,128)S(1)} %get-tuple-element.8, f32[3,1024]{1,0:T(4,128)S(1)} %get-tuple-element.9, f32[3,1024]{1,0:T(4,128)S(1)} %get-tuple-element.7), kind=kLoop, calls=%fused_computation.4 | loop fusion | flops 14155776 | bytes 33067008 | tf_op jit(solution)/shard_map/convert_element_type | solution.py:107
  109.7 2.2 copy-done.3
  111.9 1.5 multiply_convert_fusion.4
  113.4 0.0 all-to-all-done.1
  113.4 1.1 copy-done.7
  114.6 7.2 %all-to-all-start = ((bf16[16,64,768]{2,1,0:T(8,128)(2,1)}), bf16[16,64,768]{2,1,0:T(8,128)(2,1)S(1)}, u32[]{:S(2)}, u32[]{:S(2)}) async-start(bf16[16,64,768]{2,1,0:T(8,128)(2,1)} %bitcast.147), calls=%async_computation | async-start | bytes 3145728 | tf_op jit(solution)/shard_map/all_to_all | solution.py:124
  121.7 0.6 all-gather.2.cloned.1.call-start
  122.3 3.5 copy.37
  125.8 3.7 reshape.134
  129.5 4.3 fusion.92
  133.9 2.8 fusion.97
  136.6 9.2 %fusion.10 = f32[64,96,256]{2,1,0:T(8,128)} fusion(f32[96,64,256]{2,0,1:T(8,128)S(1)} %fusion.97, f32[96,64,256]{2,0,1:T(8,128)S(1)} %fusion.92, f32[96,256]{1,0:T(8,128)S(1)} %get-tuple-element.12, f32[96,256]{1,0:T(8,128)S(1)} %get-tuple-element.13), kind=kOutput, calls=%fused_computation.15 | convolution fusion | flops 4839047168 | bytes 19070976 | tf_op jit(solution)/shard_map/ckm,mj->ckj/dot_general | solution.py:27
  145.9 9.3 %fusion.6 = f32[64,96,256]{2,1,0:T(8,128)} fusion(f32[96,64,256]{2,0,1:T(8,128)S(1)} %fusion.97, f32[96,64,256]{2,0,1:T(8,128)S(1)} %fusion.92, f32[96,256]{1,0:T(8,128)S(1)} %get-tuple-element.12, f32[96,256]{1,0:T(8,128)S(1)} %get-tuple-element.13), kind=kOutput, calls=%fused_computation.11 | convolution fusion | flops 4839047168 | bytes 19070976 | tf_op jit(solution)/shard_map/ckm,mj->ckj/dot_general | solution.py:27
  155.2 9.1 %fusion.8 = f32[64,96,256]{2,1,0:T(8,128)} fusion(f32[96,64,256]{2,0,1:T(8,128)S(1)} %fusion.97, f32[96,64,256]{2,0,1:T(8,128)S(1)} %fusion.92, f32[96,256]{1,0:T(8,128)S(1)} %get-tuple-element.12, f32[96,256]{1,0:T(8,128)S(1)} %get-tuple-element.13), kind=kOutput, calls=%fused_computation.13 | convolution fusion | flops 4839047168 | bytes 19070976 | tf_op jit(solution)/shard_map/ckm,mj->ckj/dot_general | solution.py:27
  164.4 0.0 all-to-all-done
  164.4 2.0 copy.36
  166.4 3.9 reshape.132
  170.3 4.4 fusion.94
  174.7 2.7 fusion.99
  177.5 9.2 %fusion.37 = f32[64,96,256]{2,1,0:T(8,128)} fusion(f32[64,256,96]{1,2,0:T(8,128)S(1)} %fusion.99, f32[64,256,96]{1,2,0:T(8,128)S(1)} %fusion.94, f32[96,256]{1,0:T(8,128)S(1)} %get-tuple-element.12, f32[96,256]{1,0:T(8,128)S(1)} %get-tuple-element.13), kind=kOutput, calls=%fused_computation.59 | convolution fusion | flops 4839047168 | bytes 19070976 | tf_op jit(solution)/shard_map/ckm,mj->ckj/dot_general | solution.py:27
  186.7 9.6 %fusion.41 = f32[64,96,256]{2,1,0:T(8,128)} fusion(f32[64,256,96]{1,2,0:T(8,128)S(1)} %fusion.99, f32[64,256,96]{1,2,0:T(8,128)S(1)} %fusion.94, f32[96,256]{1,0:T(8,128)S(1)} %get-tuple-element.12, f32[96,256]{1,0:T(8,128)S(1)} %get-tuple-element.13), kind=kOutput, calls=%fused_computation.61 | convolution fusion | flops 4839047168 | bytes 19070976 | tf_op jit(solution)/shard_map/ckm,mj->ckj/dot_general | solution.py:27
  196.2 9.3 %fusion.39 = f32[64,96,256]{2,1,0:T(8,128)} fusion(f32[64,256,96]{1,2,0:T(8,128)S(1)} %fusion.99, f32[64,256,96]{1,2,0:T(8,128)S(1)} %fusion.94, f32[96,256]{1,0:T(8,128)S(1)} %get-tuple-element.12, f32[96,256]{1,0:T(8,128)S(1)} %get-tuple-element.13), kind=kOutput, calls=%fused_computation.60 | convolution fusion | flops 4839047168 | bytes 19070976 | tf_op jit(solution)/shard_map/ckm,mj->ckj/dot_general | solution.py:27
  205.5 9.2 %fusion.35 = f32[64,96,256]{2,1,0:T(8,128)} fusion(f32[64,256,96]{1,2,0:T(8,128)S(1)} %fusion.99, f32[64,256,96]{1,2,0:T(8,128)S(1)} %fusion.94, f32[96,256]{1,0:T(8,128)S(1)} %get-tuple-element.12, f32[96,256]{1,0:T(8,128)S(1)} %get-tuple-element.13), kind=kOutput, calls=%fused_computation.58 | convolution fusion | flops 4839047168 | bytes 19070976 | tf_op jit(solution)/shard_map/ckm,mj->ckj/dot_general | solution.py:27
  214.7 24.4 %multiply_subtract_fusion = (f32[64,96,256]{2,1,0:T(8,128)}, f32[64,96,256]{2,1,0:T(8,128)}) fusion(f32[64,96,256]{2,1,0:T(8,128)} %fusion.8, f32[64,96,256]{2,1,0:T(8,128)} %fusion.35, f32[64,96,256]{2,1,0:T(8,128)} %fusion.39, f32[64,96,256]{2,1,0:T(8,128)} %fusion.10, f32[64,96,256]{2,1,0:T(8,128)} %fusion.6, f32[64,96,256]{2,1,0:T(8,128)} %fusion.41, ...), kind=kOutput, calls=%fused_computation.33 | convolution fusion | flops 4854775808 | bytes 69402624 | tf_op jit(solution)/shard_map/ckm,mj->ckj/dot_general | solution.py:27
  239.0 0.0 slice-start.2
  239.0 9.8 %fusion.51 = f32[64,96,256]{2,1,0:T(8,128)S(1)} fusion(f32[64,96,256]{2,1,0:T(8,128)} %get-tuple-element.6), kind=kOutput, calls=%fused_computation.71 | convolution fusion | flops 4832755712 | bytes 12582912 | tf_op jit(solution)/shard_map/ckj,mj->ckm/dot_general | solution.py:27
  248.9 0.0 slice-start.3
  248.9 6.3 %fusion.57 = f32[64,96,256]{2,1,0:T(8,128)S(1)} fusion(f32[64,96,256]{2,1,0:T(8,128)S(1)} %copy-done.2), kind=kOutput, calls=%fused_computation.77 | convolution fusion | flops 4832755712 | bytes 12582912 | tf_op jit(solution)/shard_map/ckj,mj->ckm/dot_general | solution.py:27
  255.2 6.7 %fusion.49 = f32[64,96,256]{2,1,0:T(8,128)S(1)} fusion(f32[64,96,256]{2,1,0:T(8,128)S(1)} %bitcast.137), kind=kOutput, calls=%fused_computation.69 | convolution fusion | flops 4832755712 | bytes 12582912 | tf_op jit(solution)/shard_map/ckj,mj->ckm/dot_general | solution.py:27
  261.9 8.9 %fusion.59 = f32[64,96,256]{2,1,0:T(8,128)} fusion(f32[64,96,256]{2,1,0:T(8,128)S(1)} %bitcast.137), kind=kOutput, calls=%fused_computation.79 | convolution fusion | flops 4832755712 | bytes 12582912 | tf_op jit(solution)/shard_map/ckj,mj->ckm/dot_general | solution.py:27
  270.8 8.3 %fusion.14 = f32[64,256,48]{1,2,0:T(8,128)} fusion(f32[96,256]{1,0:T(8,128)S(1)} %get-tuple-element.12, f32[96,256]{1,0:T(8,128)S(1)} %get-tuple-element.13, f32[64,96,256]{2,1,0:T(8,128)S(1)} %fusion.57, f32[64,96,256]{2,1,0:T(8,128)S(1)} %fusion.49, f32[64,96,256]{2,1,0:T(8,128)} %fusion.59, f32[64,96,256]{2,1,0:T(8,128)S(1)} %fusion.51), kind=kOutput, calls=%fused_computation.24 | convolution fusion | flops 913875456 | bytes 28508160 | tf_op jit(solution)/shard_map/kn,ckm->cnm/dot_general | solution.py:27
  279.1 8.9 %multiply_bitcast_fusion = f32[64,48,256]{2,1,0:T(8,128)} fusion(f32[64,256,48]{1,2,0:T(8,128)} %fusion.14, f32[96,256]{1,0:T(8,128)S(1)} %get-tuple-element.12, f32[96,256]{1,0:T(8,128)S(1)} %get-tuple-element.13, f32[64,96,256]{2,1,0:T(8,128)S(1)} %fusion.57, f32[64,96,256]{2,1,0:T(8,128)S(1)} %fusion.49, f32[64,96,256]{2,1,0:T(8,128)} %fusion.59, ...), kind=kOutput, calls=%fused_computation.45 | convolution fusion | flops 915448320 | bytes 31653888 | tf_op jit(solution)/shard_map/kn,ckm->cnm/dot_general | solution.py:27
  288.0 4.3 reshape.135
  292.3 0.3 convert_bitcast_fusion
  292.6 0.3 copy.42
  292.9 1.2 copy-done.6
  294.2 0.3 add_convert_fusion.1
  294.5 10.0 %copy.39 = bf16[1,64,12288]{1,0,2:T(2,128)(2,1)} copy(bf16[1,64,12288]{2,1,0:T(8,128)(2,1)S(1)} %add_convert_fusion.1) | data formatting | bytes 3145728 | tf_op jit(solution)/shard_map/convert_element_type | solution.py:130
  304.5 0.5 broadcast.134
  305.0 67.2 %reduce = bf16[12288,64]{1,0:T(8,128)(2,1)S(1)} reduce(bf16[12288,1,64]{2,1,0:T(2,128)(2,1)} %bitcast.139, bf16[]{:T(256)} %broadcast.134), dimensions={1}, to_apply=%bitcast.115.reduce_sub_computation | reduce | bytes 3145730
  372.1 3.2 reshape.144
  375.4 42.1 %all_to_all.39 = bf16[16,2,24576]{2,1,0:T(2,128)(2,1)S(1)} all-to-all(bf16[16,2,24576]{2,1,0:T(2,128)(2,1)} %reshape.144), channel_id=1, replica_groups=mesh['ctx'=16,'tp'=2] {'ctx'}, dimensions={0} | all-to-all | bytes 3145728 | tf_op jit(solution)/shard_map/all_to_all | solution.py:131
  417.5 7.8 %reshape.145 = bf16[12288,1,64]{2,1,0:T(2,128)(2,1)} reshape(bf16[16,2,24576]{2,1,0:T(2,128)(2,1)S(1)} %all_to_all.39) | data formatting | bytes 3145728
  425.3 11.9 %copy.40 = bf16[1,64,12288]{2,1,0:T(8,128)(2,1)S(1)} copy(bf16[1,64,12288]{1,0,2:T(2,128)(2,1)} %bitcast.140) | data formatting | bytes 3145728 | tf_op jit(solution)/shard_map/all_to_all | solution.py:131
  437.2 0.4 copy.43
  437.7 0.2 bitcast_bitcast_fusion
  437.9 1.8 copy.41
  439.7 3.2 fusion.25
  443.0 0.0 all-gather.2.cloned.1.call-update
  443.0 45.5 %all-gather.2.cloned.1.call-done = bf16[2048,768]{1,0:T(8,128)(2,1)} async-done(((bf16[1024,768]{1,0:T(8,128)(2,1)}), bf16[2048,768]{1,0:T(8,128)(2,1)}) %all-gather.2.cloned.1.call-update) | async-done | bytes 3145744 | tf_op jit(solution)/shard_map/all_gather | solution.py:138
  488.5 13.0 %add_convert_fusion = bf16[768,2048]{1,0:T(8,128)(2,1)} fusion(f32[768,4096]{1,0:T(8,128)} %get-tuple-element.11, s32[]{:T(128)S(6)} %select_n.86, bf16[2048,768]{1,0:T(8,128)(2,1)} %all-gather.2.cloned.1.call-done, bf16[2048,2048]{1,0:T(8,128)(2,1)} %param.15), kind=kOutput, calls=%fused_computation.23 | convolution fusion | flops 6445596672 | bytes 20971524 | tf_op jit(solution)/shard_map/dot_general | solution.py:137
  (27 shorter events, 0.1 us)
Async XLA Ops:
  6.5 106.9 %all-to-all-start.1 = ((bf16[16,64,768]{2,1,0:T(8,128)(2,1)}), bf16[16,64,768]{2,1,0:T(8,128)(2,1)S(1)}, u32[]{:S(2)}, u32[]{:S(2)}) async-start(bf16[16,64,768]{2,1,0:T(8,128)(2,1)} %bitcast.149), calls=%async_computation.1 | async-start | bytes 3145728 | tf_op jit(solution)/shard_map/all_to_all | solution.py:125
  22.7 33.5 %copy-start.9 = (f32[4096]{0:T(1024)S(1)}, f32[4096]{0:T(1024)}, u32[]{:S(2)}) copy-start(f32[4096]{0:T(1024)} %param.10) | copy-start | bytes 49156
  84.1 11.0 %copy-start.8 = (f32[3,3,1024]{2,1,0:T(4,128)S(1)}, f32[3,3,1024]{2,1,0:T(4,128)}, u32[]{:S(2)}) copy-start(f32[3,3,1024]{2,1,0:T(4,128)} %param.12) | copy-start | bytes 110596
  92.5 3.8 collective-permute-start
  109.6 2.2 copy-start.3
  113.4 1.1 copy-start.7
  114.6 49.8 %all-to-all-start = ((bf16[16,64,768]{2,1,0:T(8,128)(2,1)}), bf16[16,64,768]{2,1,0:T(8,128)(2,1)S(1)}, u32[]{:S(2)}, u32[]{:S(2)}) async-start(bf16[16,64,768]{2,1,0:T(8,128)(2,1)} %bitcast.147), calls=%async_computation | async-start | bytes 3145728 | tf_op jit(solution)/shard_map/all_to_all | solution.py:124
  121.7 366.7 %all-gather.2.cloned.1.call-start = ((), (), s32[]{:S(2)}) async-start(), calls=%async_computation.3 | async-start | bytes 4718592 | tf_op jit(solution)/shard_map/all_gather | solution.py:138
  129.5 4.3 copy-start.4
  133.8 21.4 %copy-start = (f32[96,64,256]{2,0,1:T(8,128)}, f32[96,64,256]{2,0,1:T(8,128)S(1)}, u32[]{:S(2)}) copy-start(f32[96,64,256]{2,0,1:T(8,128)S(1)} %fusion.92) | copy-start | bytes 18874372
  136.6 18.6 %copy-start.1 = (f32[96,64,256]{2,0,1:T(8,128)}, f32[96,64,256]{2,0,1:T(8,128)S(1)}, u32[]{:S(2)}) copy-start(f32[96,64,256]{2,0,1:T(8,128)S(1)} %fusion.97) | copy-start | bytes 18874372
  170.3 4.4 copy-start.5
  196.2 18.4 %slice-start = ((s8[6291456]{0:T(1024)(128)(4,1)}), s8[4194304]{0:T(1024)(128)(4,1)S(1)}, s32[]{:S(2)}) async-start(s8[6291456]{0:T(1024)(128)(4,1)} %bitcast.134), calls=%async_computation.4 | async-start | bytes 8388608
  205.5 9.2 %slice-start.1 = ((s8[6291456]{0:T(1024)(128)(4,1)}), s8[2097152]{0:T(1024)(128)(4,1)S(1)}, s32[]{:S(2)}) async-start(s8[6291456]{0:T(1024)(128)(4,1)} %bitcast.134), calls=%async_computation.5 | async-start | bytes 4194304
  239.0 9.8 %copy-start.2 = (f32[64,96,256]{2,1,0:T(8,128)S(1)}, f32[64,96,256]{2,1,0:T(8,128)}, u32[]{:S(2)}) copy-start(f32[64,96,256]{2,1,0:T(8,128)} %get-tuple-element.6) | copy-start | bytes 18874372
  239.0 16.1 %slice-start.2 = ((s8[6291456]{0:T(1024)(128)(4,1)}), s8[4194304]{0:T(1024)(128)(4,1)S(1)}, s32[]{:S(2)}) async-start(s8[6291456]{0:T(1024)(128)(4,1)} %bitcast.136), calls=%async_computation.6 | async-start | bytes 8388608
  248.9 6.3 %slice-start.3 = ((s8[6291456]{0:T(1024)(128)(4,1)}), s8[2097152]{0:T(1024)(128)(4,1)S(1)}, s32[]{:S(2)}) async-start(s8[6291456]{0:T(1024)(128)(4,1)} %bitcast.136), calls=%async_computation.7 | async-start | bytes 4194304
  292.3 1.9 copy-start.6
Sparse Core Ops, SparseCore 0:
  443.1 45.3 all-gather.1
where the time goes:
time: 516 us; the launch traced here: 509 us
  matrix products  202 us (39%)
  local copies, waits for them, and re-layouts  101 us (20%)
  other arithmetic  85.9 us (17%)
  waiting for transfers between devices  45.5 us (9%)
  blocking collectives  42.1 us (8%)
  starting transfers between devices  17.7 us (3%)
  between operations  13.9 us (3%)
    dot_general x18, matrix products, contract(): jnp.einsum(form, left, right, precision=lax.Precision.HIGHEST, preferred_...  152 us
    unnamed x4, other arithmetic  67.5 us
    unnamed x33, local copies, waits for them, and re-layouts  50.2 us
    all_gather x1, waiting for transfers between devices, local(): lax.all_gather(gated, 'tp', axis=0, tiled=True)  45.5 us
    all_to_all x1, blocking collectives, local(): lax.all_to_all(outgoing.reshape(1, owned, -1), 'ctx', split_axis=2, conca...  42.1 us
    dot_general x1, matrix products, local(): jnp.dot(normed, w_in.reshape(width, 3 * chan_part), preferred_element_typ...  27.9 us
    dot_general x1, matrix products, local(): jnp.dot(lax.all_gather(gated, 'tp', axis=0, tiled=True).T, w_out, preferr...  13 us
    all_to_all x1, local copies, waits for them, and re-layouts, local(): lax.all_to_all(outgoing.reshape(1, owned, -1), 'ctx', split_axis=2, conca...  11.9 us
  transfers between devices with their start and end apart: 4, of which 1 were waited for; matrix products, arithmetic and copies ran while one was open for 27% of the time, Pallas kernels for 0%

commit v1 on v0

--- a/solution.py
+++ b/solution.py
@@ -3,8 +3,18 @@
 import jax.numpy as jnp
 from jax import lax
 from jax.sharding import PartitionSpec as P
+from jax.lax import all_to_all, axis_size
 
 norm_eps = 1e-06
+
+
+def enter_groups_by_axis(mine):
+    b_next = axis_size("ctx")
+    tmp = jnp.split(mine, b_next, axis=2)
+    local_now = jnp.stack(tmp)
+    t1 = all_to_all(local_now, split_axis=0, concat_axis=0, axis_name="ctx")
+    moved = jnp.concatenate(t1, axis=0)
+    return moved
 
 
 def shifted(block, axis, distance):
@@ -128,9 +138,7 @@
     filter_full = arrived[1].reshape(owned, -1)
     convolved = causal_conv(product, filter_full)
     outgoing = (convolved + own_skip * product.astype(jnp.float32)).astype(jnp.bfloat16)
-    returned = lax.all_to_all(
-        outgoing.reshape(1, owned, -1), "ctx", split_axis=2, concat_axis=0, tiled=True
-    )
+    returned = enter_groups_by_axis(outgoing.reshape(1, owned, -1))
     returned = returned.reshape(local_channels, positions)
     gated = (query_side.astype(jnp.float32) * returned.astype(jnp.float32)).astype(jnp.bfloat16)
     width_part = w_out.shape[1]

time: 516 us -> 412 us (0.80)
  other arithmetic: 85.9 us -> 18.4 us
  local copies, waits for them, and re-layouts: 101 us -> 65.9 us
    unnamed x4 -> x3, other arithmetic: 67.5 us -> 0.33 us
    convert_element_type x3 -> x0, local copies, waits for them, and re-layouts: 12 us -> none  [the longest x1 9.96 us: local(): (convolved + own_skip * product.astype(jnp.float32)).astype(jnp.bfloat16)]
    all_to_all x1 -> x0, local copies, waits for them, and re-layouts: 11.9 us -> none  [local(): lax.all_to_all(outgoing.reshape(1, owned, -1), 'ctx', split_axis=2, conca...]
    unnamed x33 -> x44, local copies, waits for them, and re-layouts: 50.2 us -> 38.4 us
  transfers between devices with their start and end apart: 4 -> 4, of which waited for: 1 -> 1; matrix products, arithmetic and copies ran while one was open for 27% -> 34% of each run, Pallas kernels for 0% -> 0%
where the time goes in v1:
time: 412 us; the launch traced here: 405 us
  matrix products  202 us (49%)
  local copies, waits for them, and re-layouts  65.9 us (16%)
  waiting for transfers between devices  45.5 us (11%)
  blocking collectives  41.9 us (10%)
  other arithmetic  18.4 us (4%)
  starting transfers between devices  17.4 us (4%)
  between operations  14 us (3%)
    dot_general x18, matrix products, contract(): jnp.einsum(form, left, right, precision=lax.Precision.HIGHEST, preferred_...  152 us
    all_gather x1, waiting for transfers between devices, local(): lax.all_gather(gated, 'tp', axis=0, tiled=True)  45.5 us
    all_to_all x1, blocking collectives, enter_groups_by_axis(): t1 = all_to_all(local_now, split_axis=0, concat_axis=0, axis_name='ctx')  41.9 us
    unnamed x44, local copies, waits for them, and re-layouts  38.4 us
    dot_general x1, matrix products, local(): jnp.dot(normed, w_in.reshape(width, 3 * chan_part), preferred_element_typ...  27.9 us
    dot_general x1, matrix products, local(): jnp.dot(lax.all_gather(gated, 'tp', axis=0, tiled=True).T, w_out, preferr...  13 us
    dot_general x1, matrix products, local(): embedded = jnp.dot(one_hot, embed_table, preferred_element_type=jnp.float32)  8.78 us
  transfers between devices with their start and end apart: 4, of which 1 were waited for; matrix products, arithmetic and copies ran while one was open for 34% of the time, Pallas kernels for 0%

profile of v1, /device:TPU:0, one launch (start us, length us, event | category | flops | bytes accessed | tf_op | source)
XLA Modules:
  0.0 405.1 jit_solution(11385660098312642867)
XLA Ops:
  6.5 7.4 %all-to-all-start.1 = ((bf16[16,64,768]{2,1,0:T(8,128)(2,1)}), bf16[16,64,768]{2,1,0:T(8,128)(2,1)S(1)}, u32[]{:S(2)}, u32[]{:S(2)}) async-start(bf16[16,64,768]{2,1,0:T(8,128)(2,1)} %bitcast.199), calls=%async_computation.1 | async-start | bytes 3145728 | tf_op jit(solution)/shard_map/all_to_all | solution.py:135
  13.9 8.8 %multiply_reduce_fusion = (f32[768]{0:T(1024)S(1)}, f32[768,4096]{1,0:T(8,128)}) fusion(bf16[512,4096]{1,0:T(8,128)(2,1)} %param.9, s32[768]{0:T(1024)} %param.8), kind=kOutput, calls=%fused_computation.1 | convolution fusion | flops 3227909376 | bytes 16783360 | tf_op jit(solution)/shard_map/dot_general | solution.py:100
  22.7 33.6 %copy.36 = bf16[4096,3,1024]{0,2,1:T(8,128)(2,1)} copy(bf16[4096,3,1024]{2,0,1:T(8,128)(2,1)} %param.11) | data formatting | bytes 50331648 | tf_op args[3]
  56.3 0.0 copy-done.9
  56.3 27.9 %fusion.24 = bf16[768,3072]{1,0:T(8,128)(2,1)} fusion(bf16[4096,3072]{0,1:T(8,128)(2,1)} %bitcast.192, f32[768,4096]{1,0:T(8,128)} %get-tuple-element.11, f32[4096]{0:T(1024)S(1)} %copy-done.9, f32[768]{0:T(1024)S(1)} %add_rsqrt_fusion), kind=kOutput, calls=%fused_computation.39 | convolution fusion | flops 19339149312 | bytes 42486784 | tf_op jit(solution)/shard_map/dot_general | solution.py:105
  84.2 6.6 %copy.37 = bf16[768,3072]{0,1:T(8,128)(2,1)} copy(bf16[768,3072]{1,0:T(8,128)(2,1)} %fusion.24) | data formatting | bytes 9437184 | tf_op jit(solution)/shard_map/convert_element_type | solution.py:107
  90.9 1.4 slice.40
  92.3 0.3 copy.38
  92.6 2.5 collective-permute-start
  95.0 0.0 copy-done.8
  95.1 0.4 fusion.102
  95.5 0.8 dynamic_slice.7
  96.3 0.0 collective-permute-done
  96.3 0.4 copy.39
  96.7 4.8 %maximum_convert_fusion = f32[3,1024,770]{2,1,0:T(8,128)S(1)} fusion(bf16[3,1024,768]{2,1,0:T(8,128)(2,1)} %bitcast.194, bf16[3,1024,2]{2,1,0:T(8,128)(2,1)S(1)} %copy.39), kind=kLoop, calls=%fused_computation.38 | loop fusion | flops 9461760 | bytes 14192640 | tf_op jit(solution)/shard_map/convert_element_type | solution.py:112
  101.4 8.1 %fusion.1 = bf16[3,1024,768]{2,1,0:T(8,128)(2,1)S(1)} fusion(f32[3,1024,770]{2,1,0:T(8,128)S(1)} %maximum_convert_fusion, f32[3,1024]{1,0:T(4,128)S(1)} %get-tuple-element.8, f32[3,1024]{1,0:T(4,128)S(1)} %get-tuple-element.9, f32[3,1024]{1,0:T(4,128)S(1)} %get-tuple-element.7), kind=kLoop, calls=%fused_computation.4 | loop fusion | flops 14155776 | bytes 33067008 | tf_op jit(solution)/shard_map/convert_element_type | solution.py:117
  109.6 0.0 copy-start.3
  109.6 2.2 copy-done.3
  111.8 1.5 multiply_convert_fusion.4
  113.3 0.0 all-to-all-done.1
  113.3 1.1 copy-done.7
  114.5 7.3 %all-to-all-start = ((bf16[16,64,768]{2,1,0:T(8,128)(2,1)}), bf16[16,64,768]{2,1,0:T(8,128)(2,1)S(1)}, u32[]{:S(2)}, u32[]{:S(2)}) async-start(bf16[16,64,768]{2,1,0:T(8,128)(2,1)} %bitcast.198), calls=%async_computation | async-start | bytes 3145728 | tf_op jit(solution)/shard_map/all_to_all | solution.py:134
  121.8 0.3 all-gather.2.cloned.1.call-start
  122.1 3.4 copy.41
  125.5 3.7 reshape.130
  129.2 4.3 %fusion.108 = f32[96,64,256]{2,0,1:T(8,128)S(1)} fusion(bf16[64,48,256]{2,1,0:T(8,128)(2,1)} %reshape.130), kind=kOutput, calls=%fused_computation.134 | convolution fusion | flops 906011136 | bytes 7864320 | tf_op jit(solution)/shard_map/kn,cnm->ckm/dot_general | solution.py:37
  133.6 0.0 copy-done.4
  133.6 0.0 copy-start
  133.6 2.8 fusion.113
  136.4 0.0 copy-start.1
  136.4 9.2 %fusion.10 = f32[64,96,256]{2,1,0:T(8,128)} fusion(f32[96,64,256]{2,0,1:T(8,128)S(1)} %fusion.113, f32[96,64,256]{2,0,1:T(8,128)S(1)} %fusion.108, f32[96,256]{1,0:T(8,128)S(1)} %get-tuple-element.12, f32[96,256]{1,0:T(8,128)S(1)} %get-tuple-element.13), kind=kOutput, calls=%fused_computation.15 | convolution fusion | flops 4839047168 | bytes 19070976 | tf_op jit(solution)/shard_map/ckm,mj->ckj/dot_general | solution.py:37
  145.6 9.5 %fusion.6 = f32[64,96,256]{2,1,0:T(8,128)} fusion(f32[96,64,256]{2,0,1:T(8,128)S(1)} %fusion.113, f32[96,64,256]{2,0,1:T(8,128)S(1)} %fusion.108, f32[96,256]{1,0:T(8,128)S(1)} %get-tuple-element.12, f32[96,256]{1,0:T(8,128)S(1)} %get-tuple-element.13), kind=kOutput, calls=%fused_computation.11 | convolution fusion | flops 4839047168 | bytes 19070976 | tf_op jit(solution)/shard_map/ckm,mj->ckj/dot_general | solution.py:37
  155.1 0.0 copy-done
  155.1 0.0 copy-done.1
  155.1 9.2 %fusion.8 = f32[64,96,256]{2,1,0:T(8,128)} fusion(f32[96,64,256]{2,0,1:T(8,128)S(1)} %fusion.113, f32[96,64,256]{2,0,1:T(8,128)S(1)} %fusion.108, f32[96,256]{1,0:T(8,128)S(1)} %get-tuple-element.12, f32[96,256]{1,0:T(8,128)S(1)} %get-tuple-element.13), kind=kOutput, calls=%fused_computation.13 | convolution fusion | flops 4839047168 | bytes 19070976 | tf_op jit(solution)/shard_map/ckm,mj->ckj/dot_general | solution.py:37
  164.2 0.0 all-to-all-done
  164.2 2.0 copy.40
  166.3 4.2 %reshape.128 = bf16[64,48,256]{2,1,0:T(8,128)(2,1)} reshape(bf16[1,64,16,768]{3,2,1,0:T(8,128)(2,1)} %copy.40) | data formatting | bytes 3145728 | tf_op jit(solution)/shard_map/reshape | solution.py:84
  170.5 4.4 %fusion.110 = f32[64,256,96]{1,2,0:T(8,128)S(1)} fusion(bf16[64,48,256]{2,1,0:T(8,128)(2,1)} %reshape.128), kind=kOutput, calls=%fused_computation.136 | convolution fusion | flops 906011136 | bytes 7864320 | tf_op jit(solution)/shard_map/kn,cnm->ckm/dot_general | solution.py:37
  174.9 2.7 fusion.115
  177.6 9.2 %fusion.37 = f32[64,96,256]{2,1,0:T(8,128)} fusion(f32[64,256,96]{1,2,0:T(8,128)S(1)} %fusion.115, f32[64,256,96]{1,2,0:T(8,128)S(1)} %fusion.110, f32[96,256]{1,0:T(8,128)S(1)} %get-tuple-element.12, f32[96,256]{1,0:T(8,128)S(1)} %get-tuple-element.13), kind=kOutput, calls=%fused_computation.58 | convolution fusion | flops 4839047168 | bytes 19070976 | tf_op jit(solution)/shard_map/ckm,mj->ckj/dot_general | solution.py:37
  186.8 9.4 %fusion.41 = f32[64,96,256]{2,1,0:T(8,128)} fusion(f32[64,256,96]{1,2,0:T(8,128)S(1)} %fusion.115, f32[64,256,96]{1,2,0:T(8,128)S(1)} %fusion.110, f32[96,256]{1,0:T(8,128)S(1)} %get-tuple-element.12, f32[96,256]{1,0:T(8,128)S(1)} %get-tuple-element.13), kind=kOutput, calls=%fused_computation.60 | convolution fusion | flops 4839047168 | bytes 19070976 | tf_op jit(solution)/shard_map/ckm,mj->ckj/dot_general | solution.py:37
  196.2 9.2 %fusion.39 = f32[64,96,256]{2,1,0:T(8,128)} fusion(f32[64,256,96]{1,2,0:T(8,128)S(1)} %fusion.115, f32[64,256,96]{1,2,0:T(8,128)S(1)} %fusion.110, f32[96,256]{1,0:T(8,128)S(1)} %get-tuple-element.12, f32[96,256]{1,0:T(8,128)S(1)} %get-tuple-element.13), kind=kOutput, calls=%fused_computation.59 | convolution fusion | flops 4839047168 | bytes 19070976 | tf_op jit(solution)/shard_map/ckm,mj->ckj/dot_general | solution.py:37
  205.4 9.2 %fusion.35 = f32[64,96,256]{2,1,0:T(8,128)} fusion(f32[64,256,96]{1,2,0:T(8,128)S(1)} %fusion.115, f32[64,256,96]{1,2,0:T(8,128)S(1)} %fusion.110, f32[96,256]{1,0:T(8,128)S(1)} %get-tuple-element.12, f32[96,256]{1,0:T(8,128)S(1)} %get-tuple-element.13), kind=kOutput, calls=%fused_computation.57 | convolution fusion | flops 4839047168 | bytes 19070976 | tf_op jit(solution)/shard_map/ckm,mj->ckj/dot_general | solution.py:37
  214.6 0.0 slice-done
  214.6 24.3 %multiply_subtract_fusion = (f32[64,96,256]{2,1,0:T(8,128)}, f32[64,96,256]{2,1,0:T(8,128)}) fusion(f32[64,96,256]{2,1,0:T(8,128)} %fusion.8, f32[64,96,256]{2,1,0:T(8,128)} %fusion.35, f32[64,96,256]{2,1,0:T(8,128)} %fusion.39, f32[64,96,256]{2,1,0:T(8,128)} %fusion.10, f32[64,96,256]{2,1,0:T(8,128)} %fusion.6, f32[64,96,256]{2,1,0:T(8,128)} %fusion.41, ...), kind=kOutput, calls=%fused_computation.33 | convolution fusion | flops 4854775808 | bytes 69402624 | tf_op jit(solution)/shard_map/ckm,mj->ckj/dot_general | solution.py:37
  238.9 0.0 slice-start.2
  238.9 10.0 %fusion.51 = f32[64,96,256]{2,1,0:T(8,128)S(1)} fusion(f32[64,96,256]{2,1,0:T(8,128)} %get-tuple-element.6), kind=kOutput, calls=%fused_computation.70 | convolution fusion | flops 4832755712 | bytes 12582912 | tf_op jit(solution)/shard_map/ckj,mj->ckm/dot_general | solution.py:37
  249.0 0.0 slice-start.3
  249.0 6.3 %fusion.57 = f32[64,96,256]{2,1,0:T(8,128)S(1)} fusion(f32[64,96,256]{2,1,0:T(8,128)S(1)} %copy-done.2), kind=kOutput, calls=%fused_computation.76 | convolution fusion | flops 4832755712 | bytes 12582912 | tf_op jit(solution)/shard_map/ckj,mj->ckm/dot_general | solution.py:37
  255.3 6.4 %fusion.49 = f32[64,96,256]{2,1,0:T(8,128)S(1)} fusion(f32[64,96,256]{2,1,0:T(8,128)S(1)} %bitcast.191), kind=kOutput, calls=%fused_computation.68 | convolution fusion | flops 4832755712 | bytes 12582912 | tf_op jit(solution)/shard_map/ckj,mj->ckm/dot_general | solution.py:37
  261.7 8.9 %fusion.59 = f32[64,96,256]{2,1,0:T(8,128)} fusion(f32[64,96,256]{2,1,0:T(8,128)S(1)} %bitcast.191), kind=kOutput, calls=%fused_computation.78 | convolution fusion | flops 4832755712 | bytes 12582912 | tf_op jit(solution)/shard_map/ckj,mj->ckm/dot_general | solution.py:37
  270.7 8.3 %fusion.14 = f32[64,256,48]{1,2,0:T(8,128)} fusion(f32[96,256]{1,0:T(8,128)S(1)} %get-tuple-element.12, f32[96,256]{1,0:T(8,128)S(1)} %get-tuple-element.13, f32[64,96,256]{2,1,0:T(8,128)S(1)} %fusion.57, f32[64,96,256]{2,1,0:T(8,128)S(1)} %fusion.49, f32[64,96,256]{2,1,0:T(8,128)} %fusion.59, f32[64,96,256]{2,1,0:T(8,128)S(1)} %fusion.51), kind=kOutput, calls=%fused_computation.24 | convolution fusion | flops 913875456 | bytes 28508160 | tf_op jit(solution)/shard_map/kn,ckm->cnm/dot_general | solution.py:37
  279.0 8.9 %multiply_bitcast_fusion = f32[64,48,256]{2,1,0:T(8,128)} fusion(f32[64,256,48]{1,2,0:T(8,128)} %fusion.14, f32[96,256]{1,0:T(8,128)S(1)} %get-tuple-element.12, f32[96,256]{1,0:T(8,128)S(1)} %get-tuple-element.13, f32[64,96,256]{2,1,0:T(8,128)S(1)} %fusion.57, f32[64,96,256]{2,1,0:T(8,128)S(1)} %fusion.49, f32[64,96,256]{2,1,0:T(8,128)} %fusion.59, ...), kind=kOutput, calls=%fused_computation.44 | convolution fusion | flops 915448320 | bytes 31653888 | tf_op jit(solution)/shard_map/kn,ckm->cnm/dot_general | solution.py:37
  287.9 4.3 %reshape.131 = f32[1,64,12288]{2,1,0:T(8,128)} reshape(f32[64,48,256]{2,1,0:T(8,128)} %multiply_bitcast_fusion) | data formatting | bytes 6291456 | tf_op jit(solution)/shard_map/reshape | solution.py:92
  292.2 0.3 convert_bitcast_fusion
  292.5 0.3 copy.43
  292.8 1.2 copy-done.6
  294.1 0.3 add_convert_fusion.1
  294.7 41.9 %all_to_all.35 = bf16[16,1,64,768]{3,2,1,0:T(8,128)(2,1)S(1)} all-to-all(bf16[16,1,64,768]{3,2,1,0:T(8,128)(2,1)S(1)} %fusion.84), channel_id=1, replica_groups=mesh['ctx'=16,'tp'=2] {'ctx'}, dimensions={0} | all-to-all | bytes 3145728 | tf_op jit(solution)/shard_map/all_to_all | solution.py:15
  336.6 2.9 fusion.25
  339.6 0.0 all-gather.2.cloned.1.call-update
  339.6 45.5 %all-gather.2.cloned.1.call-done = bf16[2048,768]{1,0:T(8,128)(2,1)} async-done(((bf16[1024,768]{1,0:T(8,128)(2,1)}), bf16[2048,768]{1,0:T(8,128)(2,1)}) %all-gather.2.cloned.1.call-update) | async-done | bytes 3145744 | tf_op jit(solution)/shard_map/all_gather | solution.py:146
  385.1 13.0 %add_convert_fusion = bf16[768,2048]{1,0:T(8,128)(2,1)} fusion(f32[768,4096]{1,0:T(8,128)} %get-tuple-element.11, s32[]{:T(128)S(6)} %select_n.86, bf16[2048,768]{1,0:T(8,128)(2,1)} %all-gather.2.cloned.1.call-done, bf16[2048,2048]{1,0:T(8,128)(2,1)} %param.15), kind=kOutput, calls=%fused_computation.23 | convolution fusion | flops 6445596672 | bytes 20971524 | tf_op jit(solution)/shard_map/dot_general | solution.py:145
  (34 shorter events, 0.2 us)
Async XLA Ops:
  6.5 106.8 %all-to-all-start.1 = ((bf16[16,64,768]{2,1,0:T(8,128)(2,1)}), bf16[16,64,768]{2,1,0:T(8,128)(2,1)S(1)}, u32[]{:S(2)}, u32[]{:S(2)}) async-start(bf16[16,64,768]{2,1,0:T(8,128)(2,1)} %bitcast.199), calls=%async_computation.1 | async-start | bytes 3145728 | tf_op jit(solution)/shard_map/all_to_all | solution.py:135
  22.7 33.6 %copy-start.9 = (f32[4096]{0:T(1024)S(1)}, f32[4096]{0:T(1024)}, u32[]{:S(2)}) copy-start(f32[4096]{0:T(1024)} %param.10) | copy-start | bytes 49156
  84.2 10.8 %copy-start.8 = (f32[3,3,1024]{2,1,0:T(4,128)S(1)}, f32[3,3,1024]{2,1,0:T(4,128)}, u32[]{:S(2)}) copy-start(f32[3,3,1024]{2,1,0:T(4,128)} %param.12) | copy-start | bytes 110596
  92.6 3.7 collective-permute-start
  109.6 2.2 copy-start.3
  113.3 1.1 copy-start.7
  114.5 49.8 %all-to-all-start = ((bf16[16,64,768]{2,1,0:T(8,128)(2,1)}), bf16[16,64,768]{2,1,0:T(8,128)(2,1)S(1)}, u32[]{:S(2)}, u32[]{:S(2)}) async-start(bf16[16,64,768]{2,1,0:T(8,128)(2,1)} %bitcast.198), calls=%async_computation | async-start | bytes 3145728 | tf_op jit(solution)/shard_map/all_to_all | solution.py:134
  121.8 263.3 %all-gather.2.cloned.1.call-start = ((), (), s32[]{:S(2)}) async-start(), calls=%async_computation.3 | async-start | bytes 4718592 | tf_op jit(solution)/shard_map/all_gather | solution.py:146
  129.2 4.3 %copy-start.4 = (bf16[64,48,256]{2,1,0:T(8,128)(2,1)S(1)}, bf16[64,48,256]{2,1,0:T(8,128)(2,1)}, u32[]{:S(2)}) copy-start(bf16[64,48,256]{2,1,0:T(8,128)(2,1)} %reshape.130) | copy-start | bytes 4718596
  133.6 21.5 %copy-start = (f32[96,64,256]{2,0,1:T(8,128)}, f32[96,64,256]{2,0,1:T(8,128)S(1)}, u32[]{:S(2)}) copy-start(f32[96,64,256]{2,0,1:T(8,128)S(1)} %fusion.108) | copy-start | bytes 18874372
  136.4 18.7 %copy-start.1 = (f32[96,64,256]{2,0,1:T(8,128)}, f32[96,64,256]{2,0,1:T(8,128)S(1)}, u32[]{:S(2)}) copy-start(f32[96,64,256]{2,0,1:T(8,128)S(1)} %fusion.113) | copy-start | bytes 18874372
  170.4 4.4 %copy-start.5 = (bf16[64,48,256]{2,1,0:T(8,128)(2,1)S(1)}, bf16[64,48,256]{2,1,0:T(8,128)(2,1)}, u32[]{:S(2)}) copy-start(bf16[64,48,256]{2,1,0:T(8,128)(2,1)} %reshape.128) | copy-start | bytes 4718596
  196.2 18.4 %slice-start = ((s8[6291456]{0:T(1024)(128)(4,1)}), s8[4194304]{0:T(1024)(128)(4,1)S(1)}, s32[]{:S(2)}) async-start(s8[6291456]{0:T(1024)(128)(4,1)} %bitcast.188), calls=%async_computation.4 | async-start | bytes 8388608
  205.4 9.2 %slice-start.1 = ((s8[6291456]{0:T(1024)(128)(4,1)}), s8[2097152]{0:T(1024)(128)(4,1)S(1)}, s32[]{:S(2)}) async-start(s8[6291456]{0:T(1024)(128)(4,1)} %bitcast.188), calls=%async_computation.5 | async-start | bytes 4194304
  238.9 10.0 %copy-start.2 = (f32[64,96,256]{2,1,0:T(8,128)S(1)}, f32[64,96,256]{2,1,0:T(8,128)}, u32[]{:S(2)}) copy-start(f32[64,96,256]{2,1,0:T(8,128)} %get-tuple-element.6) | copy-start | bytes 18874372
  238.9 16.3 %slice-start.2 = ((s8[6291456]{0:T(1024)(128)(4,1)}), s8[4194304]{0:T(1024)(128)(4,1)S(1)}, s32[]{:S(2)}) async-start(s8[6291456]{0:T(1024)(128)(4,1)} %bitcast.190), calls=%async_computation.6 | async-start | bytes 8388608
  249.0 6.3 %slice-start.3 = ((s8[6291456]{0:T(1024)(128)(4,1)}), s8[2097152]{0:T(1024)(128)(4,1)S(1)}, s32[]{:S(2)}) async-start(s8[6291456]{0:T(1024)(128)(4,1)} %bitcast.190), calls=%async_computation.7 | async-start | bytes 4194304
  292.2 1.9 copy-start.6
Sparse Core Ops, SparseCore 0:
  339.7 45.3 all-gather.1
